TPU v7x, 32 devices: a whole 2x2x4 slice. The times are simulated.
32 devices in a mesh: dom: 8 (over z, y), slab: 4 (over x, core).
Axes of the slice: x: 2, y: 2, z: 4, core: 2. Of those that a mesh axis runs over, the one named last changes fastest.
Arguments:
- particles: bfloat16 [1536, 32, 1024], P('dom', 'slab'), may hold values from -6 to 6
- refs: bfloat16 [2048, 32, 2048], P('dom', 'slab'), may hold values from -6 to 6
- orient: int32 [1536], P('dom'), may hold values from 0 to 2047, as said below
- shifts: int32 [1536, 8, 2], P('dom'), may hold values from -4 to 4
- tilt: int32 [1536], P('dom'), may hold values from 0 to 15
- wedge: float32 [16, 32, 1024], P(None, 'slab'), may hold values from 0.1 to 1
Outputs:
- new_refs: float32 [2048, 32, 2048], P('dom', 'slab')
- shift_weights: float32 [1536, 8], P('dom')
Inputs may be any that keep to these rules, and one draw needn't show every extreme that they name: `orient`: split the particles into aligned blocks of 192 (the rows of one device) and the orientations into ranges of 256. In every block at most 48 particles have orientations in any one range, and in every draw one range holds exactly 48 particles of every block.
All inputs are finite; a program needn't handle non-finite values.
Results may differ from a plain program's by a relative error of at most 0.004.
Values may be sent and summed in bfloat16 or wider, within the bound.
A program may use at most 128 MiB of HBM per device.

v0:
```python
import math
import jax
import jax.numpy as jnp
from jax import lax
from jax.sharding import PartitionSpec as P

BOX = 32
TILTS = 16
HIGH = lax.Precision.HIGHEST


def dft_table(box):
    pixel = jnp.arange(box * box, dtype=jnp.int32)
    row_y = pixel // box
    row_x = pixel % box
    phase = (row_y[:, None] * row_y[None, :] + row_x[:, None] * row_x[None, :]) % box
    angle = phase.astype(jnp.float32) * (2.0 * math.pi / box)
    return jnp.concatenate([jnp.cos(angle), -jnp.sin(angle)], axis=1).astype(jnp.bfloat16)


def factors(box):
    values = jnp.arange(-4, 5, dtype=jnp.int32)
    freq = jnp.arange(box, dtype=jnp.int32)
    phase = values[:, None] * freq[None, :] % box
    angle = phase.astype(jnp.float32) * (2.0 * math.pi / box)
    return (jnp.cos(angle), jnp.sin(angle))


def shift_bins(shifts):
    bins = (shifts[:, :, 0] + 4) * 9 + (shifts[:, :, 1] + 4)
    return (bins[:, :, None] == jnp.arange(81, dtype=jnp.int32)[None, None, :]).astype(jnp.float32)


def evaluate(cross, bins_hot, box):
    volume = box * box
    rows = cross.shape[0]
    cross_re = cross[:, :volume].reshape(rows, box, box)
    cross_im = cross[:, volume:].reshape(rows, box, box)
    cosine, sine = factors(box)
    inner_re = jnp.einsum("pyx,tx->pyt", cross_re, cosine, precision=HIGH) - jnp.einsum(
        "pyx,tx->pyt", cross_im, sine, precision=HIGH
    )
    inner_im = jnp.einsum("pyx,tx->pyt", cross_re, sine, precision=HIGH) + jnp.einsum(
        "pyx,tx->pyt", cross_im, cosine, precision=HIGH
    )
    outer_re = jnp.einsum("pyt,sy->pst", inner_re, cosine, precision=HIGH) - jnp.einsum(
        "pyt,sy->pst", inner_im, sine, precision=HIGH
    )
    every = outer_re.reshape(rows, 81)
    return jnp.einsum("pcb,pb->pc", bins_hot, every, precision=HIGH) / volume


def steer(weights, bins_hot, box):
    rows = weights.shape[0]
    cosine, sine = factors(box)
    binned = jnp.einsum("pc,pcb->pb", weights, bins_hot, precision=HIGH).reshape(rows, 9, 9)
    half_re = jnp.einsum("pst,tx->psx", binned, cosine, precision=HIGH)
    half_im = jnp.einsum("pst,tx->psx", binned, sine, precision=HIGH)
    phi_re = jnp.einsum("psx,sy->pyx", half_re, cosine, precision=HIGH) - jnp.einsum(
        "psx,sy->pyx", half_im, sine, precision=HIGH
    )
    phi_im = jnp.einsum("psx,sy->pyx", half_re, sine, precision=HIGH) + jnp.einsum(
        "psx,sy->pyx", half_im, cosine, precision=HIGH
    )
    return (phi_re.reshape(rows, box * box), phi_im.reshape(rows, box * box))


def shards(particles, refs, orient, shifts, tilt, wedge):
    count = particles.shape[0]
    planes = particles.shape[1]
    volume = particles.shape[2]
    owned = refs.shape[0]
    ncand = shifts.shape[1]
    peers = lax.axis_size("dom")
    capacity = 2 * count // peers
    slots_all = peers * capacity
    owner = orient // owned
    local = orient % owned
    owner_hot = (owner[:, None] == jnp.arange(peers, dtype=jnp.int32)[None, :]).astype(jnp.int32)
    before = jnp.cumsum(owner_hot, axis=0) - owner_hot
    rank = jnp.sum(before * owner_hot, axis=1)
    slot = owner * capacity + rank
    holder = (
        jnp.full((slots_all,), count, jnp.int32).at[slot].set(jnp.arange(count, dtype=jnp.int32))
    )
    meta = jnp.concatenate(
        [local[:, None], tilt[:, None], shifts.reshape(count, 2 * ncand)], axis=1
    )
    out_rows = jnp.take(particles, holder, axis=0, mode="fill", fill_value=0).reshape(
        peers, capacity, planes, volume
    )
    out_meta = jnp.take(meta, holder, axis=0, mode="fill", fill_value=-1).reshape(
        peers, capacity, 2 * ncand + 2
    )
    in_rows, in_meta = (
        lax.all_to_all(out_rows, "dom", split_axis=0, concat_axis=0, tiled=True),
        lax.all_to_all(out_meta, "dom", split_axis=0, concat_axis=0, tiled=True),
    )
    in_meta = in_meta.reshape(slots_all, 2 * ncand + 2)
    asked_local = in_meta[:, 0]
    safe = jnp.where(asked_local < 0, owned, asked_local)
    fetched = jnp.take(refs, safe, axis=0, mode="fill", fill_value=0)
    work_rows = in_rows.reshape(slots_all, planes, volume)
    work_shifts = in_meta[:, 2:].reshape(slots_all, ncand, 2)
    work_tilt = in_meta[:, 1]
    rows_here = work_rows.shape[0]
    bins_hot = shift_bins(work_shifts)
    table = dft_table(BOX)
    spectrum = jnp.dot(
        work_rows.reshape(rows_here * planes, volume), table, preferred_element_type=jnp.float32
    ).reshape(rows_here, planes, 2 * volume)
    spec_re = spectrum[:, :, :volume]
    spec_im = spectrum[:, :, volume:]
    ref_re = fetched[:, :, :volume].astype(jnp.float32)
    ref_im = fetched[:, :, volume:].astype(jnp.float32)
    cross = jnp.concatenate(
        [
            jnp.sum(spec_re * ref_re + spec_im * ref_im, axis=1),
            jnp.sum(spec_im * ref_re - spec_re * ref_im, axis=1),
        ],
        axis=1,
    )
    summed = lax.psum(cross, "slab")
    corr = evaluate(summed, bins_hot, BOX)
    score = corr / math.sqrt(BOX)
    square = score * score
    weights_here = square / (4.0 + jnp.sum(square, axis=1, keepdims=True))
    mass = jnp.sum(weights_here, axis=1)
    phi_re, phi_im = steer(weights_here, bins_hot, BOX)
    tilt_hot = (work_tilt[:, None] == jnp.arange(TILTS, dtype=jnp.int32)[None, :]).astype(
        jnp.float32
    )
    wedge_flat = wedge.reshape(TILTS, planes * volume)
    wedge_rows = jnp.dot(tilt_hot, wedge_flat, precision=HIGH).reshape(rows_here, planes, volume)
    part_re = wedge_rows * (phi_re[:, None, :] * spec_re - phi_im[:, None, :] * spec_im)
    part_im = wedge_rows * (phi_re[:, None, :] * spec_im + phi_im[:, None, :] * spec_re)
    contrib = jnp.concatenate([part_re, part_im], axis=2).astype(jnp.bfloat16)
    picker = asked_local[None, :] == jnp.arange(owned, dtype=jnp.int32)[:, None]
    picker_float = picker.astype(jnp.float32)
    incoming = contrib.reshape(slots_all, planes * 2 * volume)
    volumes = (wedge_rows * mass[:, None, None]).reshape(slots_all, planes * volume)
    acc_weight = jnp.dot(picker_float, volumes, precision=HIGH)
    back = lax.all_to_all(
        weights_here.reshape(peers, capacity, ncand), "dom", split_axis=0, concat_axis=0, tiled=True
    )
    shift_weights = jnp.take(back.reshape(slots_all, ncand), slot, axis=0)
    acc_spec = jnp.dot(
        picker.astype(jnp.bfloat16), incoming, preferred_element_type=jnp.float32
    ).reshape(owned, planes, 2 * volume)
    acc_weight = acc_weight.reshape(owned, planes, volume)
    denom = acc_weight + 1.0
    fresh = jnp.concatenate(
        [acc_spec[:, :, :volume] / denom, acc_spec[:, :, volume:] / denom], axis=2
    )
    sumsq = lax.psum(jnp.sum(fresh * fresh, axis=(1, 2)), "slab")
    rms = jnp.sqrt(sumsq / (BOX * volume))
    new_refs = fresh / jnp.maximum(rms, 1.0)[:, None, None]
    return (new_refs, shift_weights)


def solution(mesh):
    placed = (
        P("dom", "slab", None),
        P("dom", "slab", None),
        P("dom"),
        P("dom", None, None),
        P("dom"),
        P(None, "slab", None),
    )
    return jax.shard_map(
        shards,
        mesh=mesh,
        in_specs=placed,
        out_specs=(P("dom", "slab", None), P("dom", None)),
        check_vma=False,
    )
```

profile of v0, /device:TPU:0, one launch (start us, length us, event | category | flops | bytes accessed | tf_op | source)
XLA Modules:
  0.0 486.5 jit_solution(16897787885077994967)
XLA Ops:
  14.4 7.3 %all-to-all-start = ((s32[8,1,864]{2,1,0:T(1,128)}), s32[8,1,864]{2,1,0:T(1,128)S(1)}, u32[]{:S(2)}, u32[]{:S(2)}) async-start(s32[8,1,864]{2,1,0:T(1,128)} %reshape.216), calls=%async_computation | async-start | bytes 57344 | tf_op jit(solution)/shard_map/all_to_all | solution.py:97
  21.7 13.2 %gather_fusion.1 = bf16[384,8,1024]{2,1,0:T(8,128)(2,1)} fusion(bf16[192,8,1024]{2,1,0:T(8,128)(2,1)S(1)} %copy-done, s32[1024]{0:T(1024)S(1)} %pad_clamp_fusion.2), kind=kCustom, calls=%fused_computation.1 | custom fusion | bytes 12584448 | tf_op jit(solution)/shard_map/jit(_take)/gather | solution.py:89
  34.9 3.8 broadcast_select_fusion
  38.7 6.4 %copy.66 = bf16[8,48,8,1024]{3,1,2,0:T(8,128)(2,1)} copy(bf16[8,48,8,1024]{3,2,1,0:T(8,128)(2,1)S(1)} %broadcast_select_fusion) | data formatting | bytes 12582912 | tf_op jit(solution)/shard_map/jit(_take)/select_n | solution.py:89
  45.1 6.0 %all-to-all-start.1 = ((bf16[8,48,8,1024]{3,1,2,0:T(8,128)(2,1)}), bf16[8,48,8,1024]{3,1,2,0:T(8,128)(2,1)}, u32[]{:S(2)}, u32[]{:S(2)}) async-start(bf16[8,48,8,1024]{3,1,2,0:T(8,128)(2,1)} %copy.66), calls=%async_computation.1 | async-start | bytes 12582912 | tf_op jit(solution)/shard_map/all_to_all | solution.py:96
  51.2 19.0 %cosine_convert_fusion = (bf16[1024,1024]{1,0:T(8,128)(2,1)S(1)}, bf16[1024,1024]{1,0:T(8,128)(2,1)}) fusion(s32[1024]{0:T(1024)S(1)} %get-tuple-element.31, s32[1024]{0:T(1024)S(1)} %get-tuple-element.32), kind=kLoop, calls=%fused_computation.39 | loop fusion | flops 19922944 | bytes 4202496 | tf_op jit(solution)/shard_map/convert.5
  71.7 14.7 %gather_fusion.2 = bf16[384,8,2048]{2,1,0:T(8,128)(2,1)} fusion(bf16[256,8,2048]{2,1,0:T(8,128)(2,1)} %param.7, s32[1024]{0:T(1024)S(1)} %pad_clamp_fusion.1), kind=kCustom, calls=%fused_computation.2 | custom fusion | bytes 25167360 | tf_op jit(solution)/shard_map/jit(_take)/gather | solution.py:102
  86.4 23.6 %copy_select_fusion = bf16[384,8,2048]{2,0,1:T(8,128)(2,1)} fusion(bf16[384,8,2048]{2,1,0:T(8,128)(2,1)} %gather_fusion.2, pred[384]{0:T(512)(128)(4,1)S(1)} %get-tuple-element.18), kind=kLoop, calls=%fused_computation.21 | loop fusion | flops 6291456 | bytes 25166208 | tf_op jit(solution)/shard_map/jit(_take)/select_n | solution.py:102
  110.0 78.8 %all-to-all-done.1 = bf16[8,48,8,1024]{3,1,2,0:T(8,128)(2,1)} async-done(((bf16[8,48,8,1024]{3,1,2,0:T(8,128)(2,1)}), bf16[8,48,8,1024]{3,1,2,0:T(8,128)(2,1)}, u32[]{:S(2)}, u32[]{:S(2)}) %all-to-all-start.1) | async-done | bytes 6291488 | tf_op jit(solution)/shard_map/all_to_all | solution.py:96
  188.8 3.7 copy.67
  192.6 18.4 %fusion.12 = f32[384,8,2048]{2,0,1:T(8,128)} fusion(bf16[384,8,1024]{2,0,1:T(8,128)(2,1)S(1)} %bitcast.130, bf16[1024,1024]{1,0:T(8,128)(2,1)} %get-tuple-element.28, bf16[1024,1024]{1,0:T(8,128)(2,1)S(1)} %get-tuple-element.27), kind=kOutput, calls=%fused_computation.35 | convolution fusion | flops 12893290496 | bytes 35651584 | tf_op jit(solution)/shard_map/dot_general | solution.py:109
  211.0 10.9 %fusion.2 = (f32[384,1024]{1,0:T(8,128)S(1)}, f32[384,1024]{1,0:T(8,128)S(1)}) fusion(f32[384,8,2048]{2,0,1:T(8,128)} %fusion.12, bf16[384,8,2048]{2,0,1:T(8,128)(2,1)S(1)} %bitcast.124), kind=kLoop, calls=%fused_computation.13 | loop fusion | flops 30670848 | bytes 40894464 | tf_op jit(solution)/shard_map/reduce_sum | solution.py:118
  221.9 2.0 pad_maximum_fusion.2
  224.2 67.4 %all-reduce.3.cloned.1.call-done = f32[384,2048]{1,0:T(8,128)} async-done(((f32[384,2048]{1,0:T(8,128)}), f32[384,2048]{1,0:T(8,128)}) %all-reduce.3.cloned.1.call-update) | async-done | bytes 3145744 | tf_op jit(solution)/shard_map/psum | solution.py:123
  291.6 3.4 fusion.139
  296.9 2.0 fusion.51
  301.3 2.2 convolution_subtract_fusion
  303.4 2.2 convolution_add_fusion
  308.5 2.1 select_reduce_fusion
  313.8 2.8 fusion.21
  317.3 5.8 %all-to-all-start.2 = ((f32[8,1,384]{2,1,0:T(1,128)}), f32[8,1,384]{2,1,0:T(1,128)S(1)}, u32[]{:S(2)}, u32[]{:S(2)}) async-start(f32[8,1,384]{2,1,0:T(1,128)} %reshape.218), calls=%async_computation.2 | async-start | bytes 24576 | tf_op jit(solution)/shard_map/all_to_all | solution.py:143
  327.3 3.0 subtract_bitcast_fusion
  331.7 18.8 %multiply_convert_fusion.1 = (bf16[384,8,1024]{2,0,1:T(8,128)(2,1)S(1)}, bf16[384,8,1024]{2,0,1:T(8,128)(2,1)S(1)}, f32[384,8,1024]{2,0,1:T(8,128)}) fusion(f32[384,8,2048]{2,0,1:T(8,128)} %fusion.12, f32[384,1024]{1,0:T(8,128)} %copy.81, f32[384,1024]{1,0:T(8,128)S(1)} %copy.77, f32[384]{0:T(512)S(1)} %get-tuple-element.16, s32[384]{0:T(512)S(1)} %get-tuple-element.13, ...), kind=kOutput, calls=%fused_computation.23 | convolution fusion | flops 638588928 | bytes 54004736 | tf_op jit(solution)/shard_map/dot_general | solution.py:134
  350.5 5.2 %pad_maximum_fusion.1 = bf16[384,8,2048]{2,0,1:T(8,128)(2,1)} fusion(bf16[384,8,1024]{2,0,1:T(8,128)(2,1)S(1)} %get-tuple-element.21, bf16[384,8,1024]{2,0,1:T(8,128)(2,1)S(1)} %get-tuple-element.20), kind=kLoop, calls=%fused_computation.16 | loop fusion | flops 25165824 | bytes 25165824 | tf_op jit(solution)/shard_map/concatenate | solution.py:137
  355.7 16.6 %copy.82 = bf16[384,8,2048]{0,2,1:T(8,128)(2,1)} copy(bf16[384,8,2048]{2,0,1:T(8,128)(2,1)} %pad_maximum_fusion.1) | data formatting | bytes 25165824 | tf_op jit(solution)/shard_map/concatenate | solution.py:137
  372.3 12.6 %copy.83 = f32[384,8,1024]{0,2,1:T(8,128)} copy(f32[384,8,1024]{2,0,1:T(8,128)} %get-tuple-element.24) | data formatting | bytes 25165824 | tf_op jit(solution)/shard_map/mul | solution.py:141
  384.9 16.8 %fusion.7 = f32[256,8,2048]{2,0,1:T(8,128)} fusion(bf16[384,8,2048]{0,2,1:T(8,128)(2,1)} %copy.82, s32[384]{0:T(512)S(1)} %get-tuple-element.12), kind=kOutput, calls=%fused_computation.19 | convolution fusion | flops 3221323776 | bytes 29361664 | tf_op jit(solution)/shard_map/dot_general | solution.py:147
  401.7 35.2 %slice_divide_fusion.1 = (f32[256,8,1024]{2,0,1:T(8,128)}, f32[256,8,1024]{2,0,1:T(8,128)}) fusion(f32[256,8,2048]{2,0,1:T(8,128)} %fusion.7, f32[384,8,1024]{0,2,1:T(8,128)} %copy.83, s32[384]{0:T(512)S(1)} %get-tuple-element.12), kind=kOutput, calls=%fused_computation.25 | convolution fusion | flops 9670066176 | bytes 46138880 | tf_op jit(solution)/shard_map/dot_general | solution.py:142
  436.8 6.8 %multiply_reduce_fusion = f32[256]{0:T(256)S(1)} fusion(f32[256,8,1024]{2,0,1:T(8,128)} %get-tuple-element.23, f32[256,8,1024]{2,0,1:T(8,128)} %get-tuple-element.22), kind=kLoop, calls=%fused_computation.6 | loop fusion | flops 12582656 | bytes 16778240 | tf_op jit(solution)/shard_map/reduce_sum | solution.py:155
  443.6 5.8 %psum.15 = f32[256]{0:T(256)S(1)} all-reduce(f32[256]{0:T(256)S(1)} %multiply_reduce_fusion), channel_id=1, replica_groups=mesh['dom'=8,'slab'=4] {'slab'}, use_global_device_ids=true, to_apply=%region_10.11 | all-reduce | flops 256 | bytes 2048 | tf_op jit(solution)/shard_map/psum | solution.py:155
  449.4 7.0 %fusion = f32[256,8,2048]{2,0,1:T(8,128)S(1)} fusion(f32[256,8,1024]{2,0,1:T(8,128)} %get-tuple-element.23, f32[256,8,1024]{2,0,1:T(8,128)} %get-tuple-element.22, f32[256]{0:T(256)S(1)} %sqrt_maximum_fusion), kind=kLoop, calls=%fused_computation.11 | loop fusion | flops 8388608 | bytes 33555456 | tf_op jit(solution)/shard_map/div | solution.py:157
  456.4 20.0 %copy.86 = f32[256,8,2048]{2,1,0:T(8,128)} copy(f32[256,8,2048]{2,0,1:T(8,128)S(1)} %fusion) | data formatting | bytes 33554432
  (91 shorter events, 28.4 us)
Async XLA Ops:
  7.2 14.5 %copy-start = (bf16[192,8,1024]{2,1,0:T(8,128)(2,1)S(1)}, bf16[192,8,1024]{2,1,0:T(8,128)(2,1)}, u32[]{:S(2)}) copy-start(bf16[192,8,1024]{2,1,0:T(8,128)(2,1)} %param.6) | copy-start | bytes 9437188
  14.4 30.8 %all-to-all-start = ((s32[8,1,864]{2,1,0:T(1,128)}), s32[8,1,864]{2,1,0:T(1,128)S(1)}, u32[]{:S(2)}, u32[]{:S(2)}) async-start(s32[8,1,864]{2,1,0:T(1,128)} %reshape.216), calls=%async_computation | async-start | bytes 57344 | tf_op jit(solution)/shard_map/all_to_all | solution.py:97
  45.1 143.7 %all-to-all-start.1 = ((bf16[8,48,8,1024]{3,1,2,0:T(8,128)(2,1)}), bf16[8,48,8,1024]{3,1,2,0:T(8,128)(2,1)}, u32[]{:S(2)}, u32[]{:S(2)}) async-start(bf16[8,48,8,1024]{3,1,2,0:T(8,128)(2,1)} %copy.66), calls=%async_computation.1 | async-start | bytes 12582912 | tf_op jit(solution)/shard_map/all_to_all | solution.py:96
  51.1 240.4 %all-reduce.3.cloned.1.call-start = ((), (), s32[]{:S(2)}) async-start(), calls=%async_computation.3 | async-start | bytes 6291456 | tf_op jit(solution)/shard_map/psum | solution.py:123
  188.8 22.2 %slice-start = ((s8[12582912]{0:T(1024)(128)(4,1)}), s8[4194304]{0:T(1024)(128)(4,1)S(1)}, s32[]{:S(2)}) async-start(s8[12582912]{0:T(1024)(128)(4,1)} %bitcast.123), calls=%async_computation.4 | async-start | bytes 8388608
  192.6 18.4 %slice-start.1 = ((s8[12582912]{0:T(1024)(128)(4,1)}), s8[4194304]{0:T(1024)(128)(4,1)S(1)}, s32[]{:S(2)}) async-start(s8[12582912]{0:T(1024)(128)(4,1)} %bitcast.123), calls=%async_computation.5 | async-start | bytes 8388608
  192.6 18.4 %slice-start.2 = ((s8[12582912]{0:T(1024)(128)(4,1)}), s8[4194304]{0:T(1024)(128)(4,1)S(1)}, s32[]{:S(2)}) async-start(s8[12582912]{0:T(1024)(128)(4,1)} %bitcast.123), calls=%async_computation.6 | async-start | bytes 8388608
  317.3 159.1 %all-to-all-start.2 = ((f32[8,1,384]{2,1,0:T(1,128)}), f32[8,1,384]{2,1,0:T(1,128)S(1)}, u32[]{:S(2)}, u32[]{:S(2)}) async-start(f32[8,1,384]{2,1,0:T(1,128)} %reshape.218), calls=%async_computation.2 | async-start | bytes 24576 | tf_op jit(solution)/shard_map/all_to_all | solution.py:143
  456.4 22.2 %copy-start.2 = (pred[192]{0:T(512)(128)(4,1)S(1)}, pred[192]{0:T(512)(128)(4,1)}, u32[]{:S(2)}) copy-start(pred[192]{0:T(512)(128)(4,1)} %get-tuple-element.14) | copy-start | bytes 580
  456.4 23.0 %copy-start.1 = (bf16[192,8,1024]{2,1,0:T(8,128)(2,1)S(1)}, bf16[192,8,1024]{2,1,0:T(8,128)(2,1)}, u32[]{:S(2)}) copy-start(bf16[192,8,1024]{2,1,0:T(8,128)(2,1)} %param.6) | copy-start | bytes 9437188
Sparse Core Ops, SparseCore 0:
  224.1 67.4 all-reduce.2
where the time goes:
time: 495 us; the launch traced here: 486 us
  waiting for transfers between devices  146 us (29%)
  matrix products  109 us (22%)
  local copies, waits for them, and re-layouts  106 us (21%)
  other arithmetic  86.2 us (17%)
  starting transfers between devices  19.1 us (4%)
  between operations  14.7 us (3%)
  blocking collectives  5.84 us (1%)
    all_to_all x1, waiting for transfers between devices, shards(): lax.all_to_all(out_rows, 'dom', split_axis=0, concat_axis=0, tiled=True)  78.8 us
    psum x1, waiting for transfers between devices, shards(): summed = lax.psum(cross, 'slab')  67.4 us
    dot_general x1, matrix products, shards(): acc_weight = jnp.dot(picker_float, volumes, precision=HIGH)  35.2 us
    select_n x2, other arithmetic, shards(): fetched = jnp.take(refs, safe, axis=0, mode='fill', fill_value=0)  23.7 us
    unnamed x20, local copies, waits for them, and re-layouts  22.5 us
    another operation x5, other arithmetic  19.7 us
    dot_general x1, matrix products, shards(): jnp.dot(tilt_hot, wedge_flat, precision=HIGH)  18.8 us
    dot_general x1, matrix products, shards(): jnp.dot(work_rows.reshape(rows_here * planes, volume), table, preferred_e...  18.4 us
  transfers between devices with their start and end apart: 4, of which 2 were waited for; matrix products, arithmetic and copies ran while one was open for 47% of the time, Pallas kernels for 0%

commit v1 on v0

--- a/solution.py
+++ b/solution.py
@@ -120,7 +120,8 @@
         ],
         axis=1,
     )
-    summed = lax.psum(cross, "slab")
+    blocks = lax.all_gather(cross, "slab", axis=0, tiled=False)
+    summed = blocks.sum(axis=0)
     corr = evaluate(summed, bins_hot, BOX)
     score = corr / math.sqrt(BOX)
     square = score * score

time: 495 us -> 515 us (1.040)
  waiting for transfers between devices: 146 us -> 160 us
  other arithmetic: 86.2 us -> 92.4 us
    all_gather x0 -> x1, waiting for transfers between devices: none -> 81 us  [shards(): blocks = lax.all_gather(cross, 'slab', axis=0, tiled=False)]
    psum x1 -> x0, waiting for transfers between devices: 67.4 us -> none  [shards(): summed = lax.psum(cross, 'slab')]
    reduce_sum x0 -> x1, other arithmetic: none -> 6.29 us  [shards(): summed = blocks.sum(axis=0)]
    unnamed x20 -> x22, local copies, waits for them, and re-layouts: 22.5 us -> 22.5 us
  transfers between devices with their start and end apart: 4 -> 4, of which waited for: 2 -> 2; matrix products, arithmetic and copies ran while one was open for 47% -> 45% of each run, Pallas kernels for 0% -> 0%
where the time goes in v1:
time: 515 us; the launch traced here: 506 us
  waiting for transfers between devices  160 us (31%)
  matrix products  109 us (21%)
  local copies, waits for them, and re-layouts  105 us (20%)
  other arithmetic  92.4 us (18%)
  starting transfers between devices  18.9 us (4%)
  between operations  15 us (3%)
  blocking collectives  6.18 us (1%)
    all_gather x1, waiting for transfers between devices, shards(): blocks = lax.all_gather(cross, 'slab', axis=0, tiled=False)  81 us
    all_to_all x1, waiting for transfers between devices, shards(): lax.all_to_all(out_rows, 'dom', split_axis=0, concat_axis=0, tiled=True)  79.1 us
    dot_general x1, matrix products, shards(): acc_weight = jnp.dot(picker_float, volumes, precision=HIGH)  35.2 us
    select_n x2, other arithmetic, shards(): fetched = jnp.take(refs, safe, axis=0, mode='fill', fill_value=0)  23.7 us
    unnamed x22, local copies, waits for them, and re-layouts  22.5 us
    another operation x5, other arithmetic  19.4 us
    dot_general x1, matrix products, shards(): jnp.dot(tilt_hot, wedge_flat, precision=HIGH)  18.8 us
    dot_general x1, matrix products, shards(): jnp.dot(work_rows.reshape(rows_here * planes, volume), table, preferred_e...  18.7 us
  transfers between devices with their start and end apart: 4, of which 2 were waited for; matrix products, arithmetic and copies ran while one was open for 45% of the time, Pallas kernels for 0%

profile of v1, /device:TPU:0, one launch (start us, length us, event | category | flops | bytes accessed | tf_op | source)
XLA Modules:
  0.0 505.9 jit_solution(11964167889138796416)
XLA Ops:
  14.4 7.3 %all-to-all-start = ((s32[8,1,864]{2,1,0:T(1,128)}), s32[8,1,864]{2,1,0:T(1,128)S(1)}, u32[]{:S(2)}, u32[]{:S(2)}) async-start(s32[8,1,864]{2,1,0:T(1,128)} %reshape.217), calls=%async_computation | async-start | bytes 57344 | tf_op jit(solution)/shard_map/all_to_all | solution.py:97
  21.7 13.2 %gather_fusion.1 = bf16[384,8,1024]{2,1,0:T(8,128)(2,1)} fusion(bf16[192,8,1024]{2,1,0:T(8,128)(2,1)S(1)} %copy-done, s32[1024]{0:T(1024)S(1)} %pad_clamp_fusion.2), kind=kCustom, calls=%fused_computation.1 | custom fusion | bytes 12584448 | tf_op jit(solution)/shard_map/jit(_take)/gather | solution.py:89
  34.9 3.8 broadcast_select_fusion
  38.7 6.4 %copy.89 = bf16[8,48,8,1024]{3,1,2,0:T(8,128)(2,1)} copy(bf16[8,48,8,1024]{3,2,1,0:T(8,128)(2,1)S(1)} %broadcast_select_fusion) | data formatting | bytes 12582912 | tf_op jit(solution)/shard_map/jit(_take)/select_n | solution.py:89
  45.1 6.0 %all-to-all-start.1 = ((bf16[8,48,8,1024]{3,1,2,0:T(8,128)(2,1)}), bf16[8,48,8,1024]{3,1,2,0:T(8,128)(2,1)}, u32[]{:S(2)}, u32[]{:S(2)}) async-start(bf16[8,48,8,1024]{3,1,2,0:T(8,128)(2,1)} %copy.89), calls=%async_computation.1 | async-start | bytes 12582912 | tf_op jit(solution)/shard_map/all_to_all | solution.py:96
  51.2 18.7 %cosine_convert_fusion = (bf16[1024,1024]{1,0:T(8,128)(2,1)S(1)}, bf16[1024,1024]{1,0:T(8,128)(2,1)}) fusion(s32[1024]{0:T(1024)S(1)} %get-tuple-element.33, s32[1024]{0:T(1024)S(1)} %get-tuple-element.34), kind=kLoop, calls=%fused_computation.39 | loop fusion | flops 19922944 | bytes 4202496 | tf_op jit(solution)/shard_map/convert.5
  71.4 14.7 %gather_fusion.2 = bf16[384,8,2048]{2,1,0:T(8,128)(2,1)} fusion(bf16[256,8,2048]{2,1,0:T(8,128)(2,1)} %param.7, s32[1024]{0:T(1024)S(1)} %pad_clamp_fusion.1), kind=kCustom, calls=%fused_computation.2 | custom fusion | bytes 25167360 | tf_op jit(solution)/shard_map/jit(_take)/gather | solution.py:102
  86.1 23.6 %copy_select_fusion = bf16[384,8,2048]{2,0,1:T(8,128)(2,1)} fusion(bf16[384,8,2048]{2,1,0:T(8,128)(2,1)} %gather_fusion.2, pred[384]{0:T(512)(128)(4,1)S(1)} %get-tuple-element.20), kind=kLoop, calls=%fused_computation.21 | loop fusion | flops 6291456 | bytes 25166208 | tf_op jit(solution)/shard_map/jit(_take)/select_n | solution.py:102
  109.8 79.1 %all-to-all-done.1 = bf16[8,48,8,1024]{3,1,2,0:T(8,128)(2,1)} async-done(((bf16[8,48,8,1024]{3,1,2,0:T(8,128)(2,1)}), bf16[8,48,8,1024]{3,1,2,0:T(8,128)(2,1)}, u32[]{:S(2)}, u32[]{:S(2)}) %all-to-all-start.1) | async-done | bytes 6291488 | tf_op jit(solution)/shard_map/all_to_all | solution.py:96
  188.8 3.7 copy.90
  192.6 18.7 %fusion.12 = f32[384,8,2048]{2,0,1:T(8,128)} fusion(bf16[384,8,1024]{2,0,1:T(8,128)(2,1)S(1)} %bitcast.132, bf16[1024,1024]{1,0:T(8,128)(2,1)} %get-tuple-element.30, bf16[1024,1024]{1,0:T(8,128)(2,1)S(1)} %get-tuple-element.29), kind=kOutput, calls=%fused_computation.35 | convolution fusion | flops 12893290496 | bytes 35651584 | tf_op jit(solution)/shard_map/dot_general | solution.py:109
  211.3 10.9 %fusion.2 = (f32[384,1024]{1,0:T(8,128)S(1)}, f32[384,1024]{1,0:T(8,128)S(1)}) fusion(f32[384,8,2048]{2,0,1:T(8,128)} %fusion.12, bf16[384,8,2048]{2,0,1:T(8,128)(2,1)S(1)} %bitcast.125), kind=kLoop, calls=%fused_computation.13 | loop fusion | flops 30670848 | bytes 40894464 | tf_op jit(solution)/shard_map/reduce_sum | solution.py:118
  222.2 2.0 pad_maximum_fusion.2
  224.5 81.0 %all-gather.3.cloned.1.call-done = f32[1536,2048]{1,0:T(8,128)} async-done(((f32[384,2048]{1,0:T(8,128)}), f32[1536,2048]{1,0:T(8,128)}) %all-gather.3.cloned.1.call-update) | async-done | bytes 12582928 | tf_op jit(solution)/shard_map/all_gather | solution.py:123
  305.5 6.3 %reduce_sum.66 = f32[384,2048]{1,0:T(8,128)S(1)} reduce(f32[4,384,2048]{2,1,0:T(8,128)} %bitcast.131, f32[]{:T(128)} %constant.165.clone.1), dimensions={0}, to_apply=%region_6.7 | reduce | flops 2359296 | bytes 15728644 | tf_op jit(solution)/shard_map/reduce_sum | solution.py:124
  311.8 2.2 fusion.139
  320.4 2.2 convolution_subtract_fusion
  322.5 2.2 convolution_add_fusion
  327.6 2.3 select_reduce_fusion
  333.1 2.8 fusion.21
  336.6 5.5 %all-to-all-start.2 = ((f32[8,1,384]{2,1,0:T(1,128)}), f32[8,1,384]{2,1,0:T(1,128)S(1)}, u32[]{:S(2)}, u32[]{:S(2)}) async-start(f32[8,1,384]{2,1,0:T(1,128)} %reshape.219), calls=%async_computation.2 | async-start | bytes 24576 | tf_op jit(solution)/shard_map/all_to_all | solution.py:144
  346.3 3.0 subtract_bitcast_fusion
  350.8 18.8 %multiply_convert_fusion.1 = (bf16[384,8,1024]{2,0,1:T(8,128)(2,1)S(1)}, bf16[384,8,1024]{2,0,1:T(8,128)(2,1)S(1)}, f32[384,8,1024]{2,0,1:T(8,128)}) fusion(f32[384,8,2048]{2,0,1:T(8,128)} %fusion.12, f32[384,1024]{1,0:T(8,128)} %copy.104, f32[384,1024]{1,0:T(8,128)S(1)} %copy.100, f32[384]{0:T(512)S(1)} %get-tuple-element.18, ...), kind=kOutput, calls=%fused_computation.23 | convolution fusion | flops 638588928 | bytes 54004736 | tf_op jit(solution)/shard_map/dot_general | solution.py:135
  369.5 5.2 %pad_maximum_fusion.1 = bf16[384,8,2048]{2,0,1:T(8,128)(2,1)} fusion(bf16[384,8,1024]{2,0,1:T(8,128)(2,1)S(1)} %get-tuple-element.23, bf16[384,8,1024]{2,0,1:T(8,128)(2,1)S(1)} %get-tuple-element.22), kind=kLoop, calls=%fused_computation.16 | loop fusion | flops 25165824 | bytes 25165824 | tf_op jit(solution)/shard_map/concatenate | solution.py:138
  374.7 16.6 %copy.105 = bf16[384,8,2048]{0,2,1:T(8,128)(2,1)} copy(bf16[384,8,2048]{2,0,1:T(8,128)(2,1)} %pad_maximum_fusion.1) | data formatting | bytes 25165824 | tf_op jit(solution)/shard_map/concatenate | solution.py:138
  391.4 12.6 %copy.106 = f32[384,8,1024]{0,2,1:T(8,128)} copy(f32[384,8,1024]{2,0,1:T(8,128)} %get-tuple-element.26) | data formatting | bytes 25165824 | tf_op jit(solution)/shard_map/mul | solution.py:142
  403.9 16.6 %fusion.7 = f32[256,8,2048]{2,0,1:T(8,128)} fusion(bf16[384,8,2048]{0,2,1:T(8,128)(2,1)} %copy.105, s32[384]{0:T(512)S(1)} %get-tuple-element.14), kind=kOutput, calls=%fused_computation.19 | convolution fusion | flops 3221323776 | bytes 29361664 | tf_op jit(solution)/shard_map/dot_general | solution.py:148
  420.5 35.2 %slice_divide_fusion.1 = (f32[256,8,1024]{2,0,1:T(8,128)}, f32[256,8,1024]{2,0,1:T(8,128)}) fusion(f32[256,8,2048]{2,0,1:T(8,128)} %fusion.7, f32[384,8,1024]{0,2,1:T(8,128)} %copy.106, s32[384]{0:T(512)S(1)} %get-tuple-element.14), kind=kOutput, calls=%fused_computation.25 | convolution fusion | flops 9670066176 | bytes 46138880 | tf_op jit(solution)/shard_map/dot_general | solution.py:143
  455.6 6.8 %multiply_reduce_fusion = f32[256]{0:T(256)S(1)} fusion(f32[256,8,1024]{2,0,1:T(8,128)} %get-tuple-element.25, f32[256,8,1024]{2,0,1:T(8,128)} %get-tuple-element.24), kind=kLoop, calls=%fused_computation.6 | loop fusion | flops 12582656 | bytes 16778240 | tf_op jit(solution)/shard_map/reduce_sum | solution.py:156
  462.4 6.2 %psum.7 = f32[256]{0:T(256)S(1)} all-reduce(f32[256]{0:T(256)S(1)} %multiply_reduce_fusion), channel_id=1, replica_groups=mesh['dom'=8,'slab'=4] {'slab'}, use_global_device_ids=true, to_apply=%region_10.11 | all-reduce | flops 256 | bytes 2048 | tf_op jit(solution)/shard_map/psum | solution.py:156
  468.6 7.0 %fusion = f32[256,8,2048]{2,0,1:T(8,128)S(1)} fusion(f32[256,8,1024]{2,0,1:T(8,128)} %get-tuple-element.25, f32[256,8,1024]{2,0,1:T(8,128)} %get-tuple-element.24, f32[256]{0:T(256)S(1)} %sqrt_maximum_fusion), kind=kLoop, calls=%fused_computation.11 | loop fusion | flops 8388608 | bytes 33555456 | tf_op jit(solution)/shard_map/div | solution.py:158
  475.6 20.0 %copy.109 = f32[256,8,2048]{2,1,0:T(8,128)} copy(f32[256,8,2048]{2,0,1:T(8,128)S(1)} %fusion) | data formatting | bytes 33554432
  (94 shorter events, 30.5 us)
Async XLA Ops:
  7.2 14.5 %copy-start = (bf16[192,8,1024]{2,1,0:T(8,128)(2,1)S(1)}, bf16[192,8,1024]{2,1,0:T(8,128)(2,1)}, u32[]{:S(2)}) copy-start(bf16[192,8,1024]{2,1,0:T(8,128)(2,1)} %param.6) | copy-start | bytes 9437188
  14.4 30.8 %all-to-all-start = ((s32[8,1,864]{2,1,0:T(1,128)}), s32[8,1,864]{2,1,0:T(1,128)S(1)}, u32[]{:S(2)}, u32[]{:S(2)}) async-start(s32[8,1,864]{2,1,0:T(1,128)} %reshape.217), calls=%async_computation | async-start | bytes 57344 | tf_op jit(solution)/shard_map/all_to_all | solution.py:97
  45.1 143.7 %all-to-all-start.1 = ((bf16[8,48,8,1024]{3,1,2,0:T(8,128)(2,1)}), bf16[8,48,8,1024]{3,1,2,0:T(8,128)(2,1)}, u32[]{:S(2)}, u32[]{:S(2)}) async-start(bf16[8,48,8,1024]{3,1,2,0:T(8,128)(2,1)} %copy.89), calls=%async_computation.1 | async-start | bytes 12582912 | tf_op jit(solution)/shard_map/all_to_all | solution.py:96
  51.1 254.4 %all-gather.3.cloned.1.call-start = ((), (), s32[]{:S(2)}) async-start(), calls=%async_computation.3 | async-start | bytes 15728640 | tf_op jit(solution)/shard_map/all_gather | solution.py:123
  188.8 22.5 %slice-start = ((s8[12582912]{0:T(1024)(128)(4,1)}), s8[4194304]{0:T(1024)(128)(4,1)S(1)}, s32[]{:S(2)}) async-start(s8[12582912]{0:T(1024)(128)(4,1)} %bitcast.124), calls=%async_computation.4 | async-start | bytes 8388608
  192.6 18.7 %slice-start.1 = ((s8[12582912]{0:T(1024)(128)(4,1)}), s8[4194304]{0:T(1024)(128)(4,1)S(1)}, s32[]{:S(2)}) async-start(s8[12582912]{0:T(1024)(128)(4,1)} %bitcast.124), calls=%async_computation.5 | async-start | bytes 8388608
  192.6 18.7 %slice-start.2 = ((s8[12582912]{0:T(1024)(128)(4,1)}), s8[4194304]{0:T(1024)(128)(4,1)S(1)}, s32[]{:S(2)}) async-start(s8[12582912]{0:T(1024)(128)(4,1)} %bitcast.124), calls=%async_computation.6 | async-start | bytes 8388608
  314.0 5.9 %copy-start.2 = (f32[384,1024]{1,0:T(8,128)S(1)}, f32[384,1024]{1,0:T(8,128)}, u32[]{:S(2)}) copy-start(f32[384,1024]{1,0:T(8,128)} %get-tuple-element.27) | copy-start | bytes 4718596
  336.6 159.0 %all-to-all-start.2 = ((f32[8,1,384]{2,1,0:T(1,128)}), f32[8,1,384]{2,1,0:T(1,128)S(1)}, u32[]{:S(2)}, u32[]{:S(2)}) async-start(f32[8,1,384]{2,1,0:T(1,128)} %reshape.219), calls=%async_computation.2 | async-start | bytes 24576 | tf_op jit(solution)/shard_map/all_to_all | solution.py:144
  475.6 22.2 %copy-start.3 = (pred[192]{0:T(512)(128)(4,1)S(1)}, pred[192]{0:T(512)(128)(4,1)}, u32[]{:S(2)}) copy-start(pred[192]{0:T(512)(128)(4,1)} %get-tuple-element.16) | copy-start | bytes 580
  475.6 23.0 %copy-start.1 = (bf16[192,8,1024]{2,1,0:T(8,128)(2,1)S(1)}, bf16[192,8,1024]{2,1,0:T(8,128)(2,1)}, u32[]{:S(2)}) copy-start(bf16[192,8,1024]{2,1,0:T(8,128)(2,1)} %param.6) | copy-start | bytes 9437188
Sparse Core Ops, SparseCore 0:
  224.4 81.1 all-gather.2
